TPU v7x, 32 devices: a whole 2x2x4 slice. The times are simulated.
32 devices in a mesh: dp: 4 (over y, x), expert: 4 (over z), tensor: 2 (over core).
Axes of the slice: x: 2, y: 2, z: 4, core: 2. Of those that a mesh axis runs over, the one named last changes fastest.
Arguments:
- out_grad: bfloat16 [2048, 2048], P(('dp', 'expert'), 'tensor'), may hold values from -6 to 6
- seq_ids: int32 [16, 128], P(('dp', 'expert')), may hold values from 0 to 3, never falling along the last dimension, each value on 1 to 64 neighbouring positions
- seq_weights: float32 [16, 4], P(('dp', 'expert')), may hold values from -1.5 to 1.5
- expert_ids: int32 [2048, 2], P(('dp', 'expert')), may hold values from 0 to 3, all different within a row; in each aligned block of 128 rows (0 to 127, 128 to 255, ...) at most 96 rows name the same one
- route_probs: bfloat16 [2048, 2], P(('dp', 'expert')), may hold values from 0.19921875 to 1
- down_weight: bfloat16 [4, 7168, 2048], P('expert', ('dp', 'tensor')), may hold values from -0.0625 to 0.0625
- gate_pre: bfloat16 [4, 7168, 1536], P('expert', ('dp', 'tensor')), may hold values from -6 to 6
- up_pre: bfloat16 [4, 7168, 1536], P('expert', ('dp', 'tensor')), may hold values from -6 to 6
Outputs:
- grad_gate: bfloat16 [4, 7168, 1536], P('expert', ('dp', 'tensor'))
- grad_up: bfloat16 [4, 7168, 1536], P('expert', ('dp', 'tensor'))
- grad_down: bfloat16 [4, 7168, 2048], P('expert', ('dp', 'tensor'))
- grad_probs: float32 [2048, 2], P(('dp', 'expert'))
Inputs may be any that keep to these rules, and one draw needn't show every extreme that they name: `expert_ids`: the two experts of a token differ. Among the 128 tokens of one shard no expert is named more than 96 times, and in every draw some expert is named exactly 96 times by the tokens of some shard. `seq_ids`: along a shard's row the ids never fall; each of the 4 ids names 1 to 64 tokens of the row, and one names exactly 64.
All inputs are finite; a program needn't handle non-finite values.
Results may differ from a plain program's by a relative error of at most 0.0064.
Values may be sent and summed in bfloat16 or wider, within the bound.
A program may use at most 128 MiB of HBM per device.

v0:
```python
import functools

import jax
import jax.numpy as jnp
from jax import lax
from jax.experimental import pallas as pl
from jax.experimental.pallas import tpu as pltpu
from jax.sharding import PartitionSpec as P

MESH = pl.DeviceIdType.MESH
LANES = 128
SUBLANES = 8


def silu_parts(pre_act):
    logistic = jax.nn.sigmoid(pre_act)
    return (pre_act * logistic, logistic * (1.0 + pre_act * (1.0 - logistic)))


def flip(index, mask):
    bit = 1
    while bit <= mask:
        if mask & bit:
            index = index + bit * (1 - 2 * lax.rem(lax.div(index, bit), 2))
        bit *= 2
    return index


class Copies:
    def __init__(self, send_sem, recv_sem):
        self.send_sem, self.recv_sem, self.made = send_sem, recv_sem, []

    def start(self, src, dst, device):
        at = len(self.made)
        copy = pltpu.make_async_remote_copy(
            src_ref=src,
            dst_ref=dst,
            send_sem=self.send_sem.at[at],
            recv_sem=self.recv_sem.at[at],
            device_id=device,
            device_id_type=MESH,
        )
        copy.start()
        self.made.append(copy)
        return copy


def greet(peers):
    barrier = pltpu.get_barrier_semaphore()
    for peer in peers:
        pl.semaphore_signal(barrier, inc=1, device_id=peer, device_id_type=MESH)
    pl.semaphore_wait(barrier, len(peers))


def copy_count(columns, experts, cores):
    probe = columns * cores + experts
    if columns == 4:
        per_block = 6 + 7 * (cores - 1)
        return (experts - 1) * 2 + (columns - 1) + experts * per_block + probe
    return (experts - 1) * 2 + (columns - 1) * 2 + columns * (cores - 1) + probe


def row_tile(rows):
    return max(tile for tile in range(16, 257, 16) if rows % tile == 0)


def moe_kernel(
    columns,
    experts,
    cores,
    rows_ref,
    probs_ref,
    weight_hbm,
    gate_hbm,
    up_hbm,
    ups_ref,
    acc_ref,
    probs_out,
    probe_out,
    gathered,
    weight_ref,
    gate_ref,
    up_ref,
    hidden_ref,
    weighted_ref,
    part_ref,
    first,
    total,
    second,
    load_sem,
    send_sem,
    recv_sem,
):
    d, e, t = lax.axis_index("dp"), lax.axis_index("expert"), lax.axis_index("tensor")
    capacity, half = rows_ref.shape[1], rows_ref.shape[2]
    group_size = experts * capacity
    units = weight_ref.shape[0]
    tile = row_tile(units)
    tiles = units // tile
    loads = [
        pltpu.make_async_copy(src, dst, load_sem.at[at])
        for at, (src, dst) in enumerate(
            ((gate_hbm, gate_ref), (up_hbm, up_ref), (weight_hbm, weight_ref))
        )
    ]
    for load in loads:
        load.start()
    greet(
        [(d, flip(e, k), t) for k in range(1, experts)]
        + [
            (flip(d, m), e, flip(t, f))
            for m in range(columns)
            for f in range(cores)
            if m or f
        ]
    )
    copies = Copies(send_sem, recv_sem)
    base = pl.multiple_of(t * half, half)
    mine = pl.ds(base, half)
    along, small = [None], [None]
    for k in range(1, experts):
        to = (d, flip(e, k), t)
        along.append(copies.start(rows_ref.at[flip(e, k)], gathered.at[d, e, :, mine], to))
        small.append(copies.start(probs_ref.at[flip(e, k)], probs_out.at[d, e], to))
    last = [[] for _ in range(columns)]

    def to_cores(m, src, dst):
        for f in range(1, cores):
            last[m].append(copies.start(src, dst, (d, e, flip(t, f))))

    def make_hidden(at):
        if at == 0:
            loads[0].wait()
            loads[1].wait()
        span = pl.ds(at * tile, tile)
        gate = gate_ref[span, :].astype(jnp.float32)
        hidden_ref[span, :] = (gate * jax.nn.sigmoid(gate) * up_ref[span, :].astype(jnp.float32)).astype(
            jnp.bfloat16
        )

    def some_hidden(k):
        for at in range(k * tiles // experts, (k + 1) * tiles // experts):
            make_hidden(at)

    def spread_probs():
        for k in range(1, experts):
            small[k].wait_recv()
        group = probs_out.at[d]
        for m in range(1, columns):
            last[m].append(copies.start(group, group, (flip(d, m), e, t)))

    firsts = {}

    def compute(m):
        for copy in last[m]:
            copy.wait_recv()
        where = flip(d, m)
        cols = pl.ds(pl.multiple_of(where * group_size, 128), group_size)
        eye = lax.broadcasted_iota(jnp.int32, (capacity, capacity), 0) == lax.broadcasted_iota(
            jnp.int32, (capacity, capacity), 1
        )
        for j in range(experts):
            prob = probs_out[where, j][0:1, 0:capacity]
            diag = jnp.where(eye, prob, 0.0).astype(jnp.bfloat16)
            weighted_ref[pl.ds(j * capacity, capacity), :] = jnp.dot(
                diag, gathered[where, j], preferred_element_type=jnp.float32
            ).astype(jnp.bfloat16)

        def up_step(i, part):
            span = pl.ds(pl.multiple_of(i * tile, tile), tile)
            block = gathered[where].reshape(group_size, half * cores)
            ups = lax.dot_general(
                weight_ref[span, :], block, (((1,), (1,)), ((), ())),
                preferred_element_type=jnp.float32,
            )
            ups_ref[span, cols] = ups
            value = ups * hidden_ref[span, cols].astype(jnp.float32)
            return part + jnp.sum(value, axis=0, keepdims=True)

        part = lax.fori_loop(0, tiles, up_step, jnp.zeros((1, group_size), jnp.float32))
        part_ref[where] = jnp.broadcast_to(part, (8, group_size))
        for f in range(cores):
            if m or f:
                at = m * cores + f - 1
                firsts[at] = copies.start(
                    part_ref.at[where], first.at[at], (where, e, flip(t, f))
                )

        def down_step(i, carry):
            span = pl.ds(pl.multiple_of(i * tile, tile), tile)
            out = jnp.dot(
                hidden_ref[span, cols], weighted_ref[...], preferred_element_type=jnp.float32
            )
            acc_ref[span, :] = out if m == 0 else acc_ref[span, :] + out
            return carry

        lax.fori_loop(0, tiles, down_step, 0)

    if columns == 4:
        piece = half // 2
        cuts = [pl.ds(pl.multiple_of(base + p * piece, piece), piece) for p in range(2)]
        sent = {}

        def spread(k):
            origin = flip(e, k)
            if k > 0:
                along[k].wait_recv()
            for m, order in ((1, (0, 1)), (2, (1, 0))):
                for p in order:
                    here = gathered.at[d, origin, :, cuts[p]]
                    src = rows_ref.at[e, :, pl.ds(p * piece, piece)] if k == 0 else here
                    sent[k, m, p] = copies.start(src, here, (flip(d, m), e, t))
            whole = gathered.at[d, origin, :, mine]
            to_cores(0, rows_ref.at[e] if k == 0 else whole, whole)

        def forward(k):
            origin = flip(e, k)
            for m, p in ((1, 0), (2, 1)):
                sent[k, m, p].wait_recv()
                block = gathered.at[flip(d, m), origin, :, cuts[p]]
                sent[k, 3, p] = copies.start(block, block, (flip(d, 3 - m), e, t))
                to_cores(m, block, block)
            for m, p in ((1, 1), (2, 0)):
                sent[k, m, p].wait_recv()
                block = gathered.at[flip(d, m), origin, :, cuts[p]]
                to_cores(m, block, block)

        def finish(k):
            for p in range(2):
                sent[k, 3, p].wait_recv()
                block = gathered.at[flip(d, 3), flip(e, k), :, cuts[p]]
                to_cores(3, block, block)

        spread(0)
        gathered[d, e, :, mine] = rows_ref[e]
        probs_out[d, e] = probs_ref[e]
        some_hidden(0)
        for k in range(1, experts):
            spread(k)
            some_hidden(k)
            if k == 1:
                forward(0)
        spread_probs()
        for k in range(1, experts - 1):
            forward(k)
        loads[2].wait()
        compute(0)
        forward(experts - 1)
        compute(1)
        for k in range(experts - 1):
            finish(k)
        compute(2)
        finish(experts - 1)
        compute(3)
    else:
        gathered[d, e, :, mine] = rows_ref[e]
        probs_out[d, e] = probs_ref[e]
        for k in range(1, experts):
            along[k].wait_recv()
        group = gathered.at[d, :, :, mine]
        spreads = [copies.start(group, group, (flip(d, m), e, t)) for m in range(1, columns)]
        to_cores(0, group, group)
        spread_probs()
        for at in range(tiles):
            make_hidden(at)
        loads[2].wait()
        compute(0)
        for m in range(1, columns):
            spreads[m - 1].wait_recv()
            block = gathered.at[flip(d, m), :, :, mine]
            to_cores(m, block, block)
            compute(m)
    acc = part_ref[d]
    for at in range(columns * cores - 1):
        firsts[at].wait_recv()
        acc = acc + first[at]
    total[...] = acc
    backs = [copies.start(total, second.at[k - 1], (d, flip(e, k), t)) for k in range(1, experts)]
    probe_out[e] = acc
    for k in range(1, experts):
        backs[k - 1].wait_recv()
        probe_out[flip(e, k)] = second[k - 1]
    for copy in copies.made:
        copy.wait_send()


def local(out_grad, seq_ids, seq_weights, expert_ids, route_probs, down_weight, gate_pre, up_pre):
    experts = lax.axis_size("expert")
    columns = lax.axis_size("dp")
    cores = lax.axis_size("tensor")
    token_count = seq_ids.shape[1]
    slots = gate_pre.shape[2]
    capacity = slots // (columns * experts)
    half_width = out_grad.shape[1]
    width = half_width * cores
    seq_count = seq_weights.shape[1]
    block_size = experts * capacity
    padded = -(-capacity // LANES) * LANES
    gate_local = gate_pre[0]
    up_local = up_pre[0]
    weight_local = down_weight[0]
    member = (seq_ids[0][:, None] == jnp.arange(seq_count, dtype=jnp.int32)[None, :]).astype(
        jnp.float32
    )
    weight_tok = jnp.sum(member * seq_weights[0][None, :], axis=1)
    scaled = (weight_tok[:, None] * out_grad.astype(jnp.float32)).astype(jnp.bfloat16)
    chosen = expert_ids.reshape(-1)
    pairs = chosen.shape[0]
    onehot = chosen[:, None] == jnp.arange(experts, dtype=jnp.int32)[None, :]
    rank = jnp.arange(pairs, dtype=jnp.int32)
    lower = (rank[None, :] < rank[:, None]).astype(jnp.bfloat16)
    earlier = jnp.dot(lower, onehot.astype(jnp.bfloat16), preferred_element_type=jnp.float32)
    position = jnp.sum(jnp.where(onehot, earlier, 0.0), axis=1).astype(jnp.int32)
    slot_index = chosen * capacity + position
    filled = slot_index[None, :] == jnp.arange(block_size, dtype=jnp.int32)[:, None]
    send_probs = jnp.sum(
        jnp.where(filled, route_probs.reshape(-1).astype(jnp.float32)[None, :], 0.0), axis=1
    )
    by_token = slot_index.reshape(token_count, 2)
    every = jnp.arange(block_size, dtype=jnp.int32)[:, None]
    picks = ((by_token[:, 0][None, :] == every) | (by_token[:, 1][None, :] == every)).astype(
        jnp.bfloat16
    )
    send_rows = jnp.dot(picks, scaled, preferred_element_type=jnp.float32).astype(jnp.bfloat16)
    prob_tile = jnp.zeros((experts, SUBLANES, padded), jnp.float32)
    prob_tile = prob_tile + jnp.pad(
        send_probs.reshape(experts, 1, capacity), ((0, 0), (0, 0), (0, padded - capacity))
    )
    amount = copy_count(columns, experts, cores)
    units = weight_local.shape[0]
    anywhere = pl.BlockSpec(memory_space=pl.ANY)
    inside = pl.BlockSpec(memory_space=pltpu.VMEM)
    upstream, grad_w, probs_all, probes = pl.pallas_call(
        functools.partial(moe_kernel, columns, experts, cores),
        out_shape=(
            jax.ShapeDtypeStruct((units, slots), jnp.float32),
            jax.ShapeDtypeStruct((units, width), jnp.float32),
            jax.ShapeDtypeStruct((columns, experts, SUBLANES, padded), jnp.float32),
            jax.ShapeDtypeStruct((experts, SUBLANES, block_size), jnp.float32),
        ),
        in_specs=[inside, inside, anywhere, anywhere, anywhere],
        out_specs=[inside] * 4,
        scratch_shapes=[
            pltpu.VMEM((columns, experts, capacity, width), jnp.bfloat16),
            pltpu.VMEM((units, width), jnp.bfloat16),
            pltpu.VMEM((units, slots), jnp.bfloat16),
            pltpu.VMEM((units, slots), jnp.bfloat16),
            pltpu.VMEM((units, slots), jnp.bfloat16),
            pltpu.VMEM((block_size, width), jnp.bfloat16),
            pltpu.VMEM((columns, SUBLANES, block_size), jnp.float32),
            pltpu.VMEM((columns * cores - 1, SUBLANES, block_size), jnp.float32),
            pltpu.VMEM((SUBLANES, block_size), jnp.float32),
            pltpu.VMEM((experts - 1, SUBLANES, block_size), jnp.float32),
            pltpu.SemaphoreType.DMA((3,)),
            pltpu.SemaphoreType.DMA((amount,)),
            pltpu.SemaphoreType.DMA((amount,)),
        ],
        compiler_params=pltpu.CompilerParams(
            collective_id=0, has_side_effects=True, vmem_limit_bytes=50 * 1024 * 1024
        ),
        name="moe",
    )(send_rows.reshape(experts, capacity, half_width), prob_tile, weight_local, gate_local, up_local)
    arrived_probs = probs_all[:, :, 0, :capacity].reshape(slots)
    gate_piece = gate_local.astype(jnp.float32)
    up_piece = up_local.astype(jnp.float32)
    activated, derivative = silu_parts(gate_piece)
    grad_hidden = arrived_probs[None, :] * upstream
    gate_out = (grad_hidden * up_piece * derivative).astype(jnp.bfloat16)
    up_out = (grad_hidden * activated).astype(jnp.bfloat16)
    grad_w = grad_w.astype(jnp.bfloat16)
    own = lax.dynamic_slice_in_dim(
        probes[:, 0, :], lax.axis_index("expert") * capacity, capacity, 1
    )
    returned = own.reshape(-1)
    grad_probs = jnp.sum(jnp.where(filled, returned[:, None], 0.0), axis=0).reshape(token_count, 2)
    return (gate_out[None], up_out[None], grad_w[None], grad_probs)


def solution(mesh):
    return jax.shard_map(
        local,
        mesh=mesh,
        in_specs=(
            P(("dp", "expert"), "tensor"),
            P(("dp", "expert"), None),
            P(("dp", "expert"), None),
            P(("dp", "expert"), None),
            P(("dp", "expert"), None),
            P("expert", ("dp", "tensor"), None),
            P("expert", ("dp", "tensor"), None),
            P("expert", ("dp", "tensor"), None),
        ),
        out_specs=(
            P("expert", ("dp", "tensor"), None),
            P("expert", ("dp", "tensor"), None),
            P("expert", ("dp", "tensor"), None),
            P(("dp", "expert"), None),
        ),
        check_vma=False,
    )
```

profile of v0, /device:TPU:0, one launch (start us, length us, event | category | flops | bytes accessed | tf_op | source)
XLA Modules:
  0.0 88.4 jit_solution(43580929101400311)
XLA Ops:
  0.6 0.8 copy.27
  1.4 0.1 eq.73
  1.6 0.2 fusion.11
  1.8 0.1 convert_element_type.52
  1.9 0.1 copy.28
  2.0 0.7 multiply_add_fusion.1
  2.7 0.8 select_reduce_fusion.2
  3.4 1.4 %convolution_convert_fusion = bf16[384,1024]{1,0:T(8,128)(2,1)S(1)} fusion(bf16[128,1024]{1,0:T(8,128)(2,1)} %param.8, f32[128]{0:T(128)S(1)} %select_reduce_fusion.2, s32[128]{0:T(128)S(1)} %get-tuple-element.31, s32[128]{0:T(128)S(1)} %get-tuple-element.30), kind=kOutput, calls=%fused_computation.15 | convolution fusion | flops 101597184 | bytes 1050112 | tf_op jit(solution)/shard_map/dot_general | solution.py:324
  4.9 0.8 copy.29
  5.6 0.1 reshape.50
  5.8 0.2 select_reduce_fusion.1
  5.9 0.1 reshape.48
  6.0 1.8 %copy-done = bf16[1,896,1536]{2,1,0:T(8,128)(2,1)S(1)} copy-done((bf16[1,896,1536]{2,1,0:T(8,128)(2,1)S(1)}, bf16[1,896,1536]{2,1,0:T(8,128)(2,1)}, u32[]{:S(2)}) %copy-start) | copy-done | bytes 2752536
  7.8 65.8 %moe.1 = (f32[896,1536]{1,0:T(8,128)}, f32[896,2048]{1,0:T(8,128)}, f32[4,4,8,128]{3,2,1,0:T(8,128)S(1)}, f32[4,8,384]{2,1,0:T(8,128)S(1)}) custom-call(bf16[4,96,1024]{2,1,0:T(8,128)(2,1)S(1)} %bitcast.22, f32[4,8,128]{2,1,0:T(8,128)S(1)} %add.31.probs_ref, bf16[896,2048]{1,0:T(8,128)(2,1)} %bitcast.24, bf16[896,1536]{1,0:T(8,128)(2,1)S(1)} %bitcast.21, ...), custom_call_target="tpu_custom_call" | custom-call | tf_op jit(solution)/shard_map/moe/pallas_call | solution.py:333
  73.7 0.6 copy-done.2
  74.3 0.1 mul.73
  74.4 6.6 %fusion.9 = (bf16[1,896,1536]{2,1,0:T(8,128)(2,1)}, bf16[1,896,1536]{2,1,0:T(8,128)(2,1)}) fusion(f32[896,1536]{1,0:T(8,128)} %get-tuple-element.9, f32[1536]{0:T(1024)S(1)} %mul.73, bf16[1,896,1536]{2,1,0:T(8,128)(2,1)S(1)} %copy-done.1, bf16[1,896,1536]{2,1,0:T(8,128)(2,1)} %param.15), kind=kLoop, calls=%fused_computation.13 | loop fusion | flops 22020096 | bytes 16521216 | tf_op jit(solution)/shard_map/broadcast_in_dim | solution.py:376
  81.0 0.8 slice.15
  81.8 0.1 dynamic-slice_reduce_fusion
  81.9 0.1 broadcast_in_dim.52
  82.0 0.1 select_reduce_fusion
  82.1 0.1 reshape.49
  82.3 0.6 copy.30
  82.9 5.5 %convert_bitcast_fusion = bf16[1,896,2048]{2,1,0:T(8,128)(2,1)} fusion(f32[896,2048]{1,0:T(8,128)} %get-tuple-element.10), kind=kLoop, calls=%fused_computation.12 | loop fusion | flops 1835008 | bytes 11010048 | tf_op jit(solution)/shard_map/broadcast_in_dim | solution.py:376
  (10 shorter events, 0.1 us)
Async XLA Ops:
  6.0 1.8 %copy-start = (bf16[1,896,1536]{2,1,0:T(8,128)(2,1)S(1)}, bf16[1,896,1536]{2,1,0:T(8,128)(2,1)}, u32[]{:S(2)}) copy-start(bf16[1,896,1536]{2,1,0:T(8,128)(2,1)} %param.14) | copy-start | bytes 8257540
  7.8 66.6 %copy-start.1 = (bf16[1,896,1536]{2,1,0:T(8,128)(2,1)S(1)}, bf16[1,896,1536]{2,1,0:T(8,128)(2,1)}, u32[]{:S(2)}) copy-start(bf16[1,896,1536]{2,1,0:T(8,128)(2,1)} %param.14) | copy-start | bytes 8257540
  73.6 0.6 copy-start.2
where the time goes:
time: 88.7 us; the launch traced here: 88.4 us
  Pallas kernels  65.8 us (74%)
  other arithmetic  13.9 us (16%)
  local copies, waits for them, and re-layouts  6.4 us (7%)
  matrix products  1.59 us (2%)
    pallas_call x1, Pallas kernels, local(): pl.pallas_call(functools.partial(moe_kernel, columns, experts, cores), ou...  65.8 us
    broadcast_in_dim x2, other arithmetic, local(): return (gate_out[None], up_out[None], grad_w[None], grad_probs)  12.1 us
    unnamed x8, local copies, waits for them, and re-layouts  3.82 us

commit v1 on v0

v1 whole, which is shorter than its diff:
```python
import functools

import jax
import jax.numpy as jnp
from jax import lax
from jax.experimental import pallas as pl
from jax.experimental.pallas import tpu as pltpu
from jax.sharding import PartitionSpec as P

MESH = pl.DeviceIdType.MESH
LANES = 128
SILU_ROWS = 16
DOWN_CHUNKS = 4


def flip(index, mask):
    bit = 1
    while bit <= mask:
        if mask & bit:
            index = index + bit * (1 - 2 * lax.rem(lax.div(index, bit), 2))
        bit *= 2
    return index


class Copies:
    def __init__(self, send_sem, recv_sem):
        self.send_sem, self.recv_sem, self.made = send_sem, recv_sem, []

    def start(self, src, dst, device):
        at = len(self.made)
        copy = pltpu.make_async_remote_copy(
            src_ref=src,
            dst_ref=dst,
            send_sem=self.send_sem.at[at],
            recv_sem=self.recv_sem.at[at],
            device_id=device,
            device_id_type=MESH,
        )
        copy.start()
        self.made.append(copy)
        return copy


def copy_count(columns, experts, cores):
    amount = (columns * experts - 1) + (experts - 1) + (columns * experts * cores - 1)
    if columns == 4:
        return amount + experts * (6 + 7 * (cores - 1))
    return amount + (columns - 1) + columns * (cores - 1)


def moe_kernel(
    columns,
    experts,
    cores,
    capacity,
    ids_ref,
    routes_ref,
    seq_ref,
    seq_weight_ref,
    grad_ref,
    weight_hbm,
    gate_hbm,
    up_hbm,
    gate_out,
    up_out,
    down_out,
    probs_out,
    gathered,
    rows_ref,
    prob_send,
    prob_in,
    weight_ref,
    gate_ref,
    up_ref,
    hidden_ref,
    gate_coef,
    up_coef,
    window_ref,
    scaled_hidden,
    acc_ref,
    part_ref,
    probe_in,
    load_sem,
    send_sem,
    recv_sem,
):
    d, e, t = lax.axis_index("dp"), lax.axis_index("expert"), lax.axis_index("tensor")
    tokens, half = grad_ref.shape
    width = half * cores
    group = experts * capacity
    units = weight_ref.shape[0]
    slots = gate_ref.shape[1]
    half_rows = group // 2
    span = -(-half_rows // LANES) * LANES
    upper = lax.div(2 * e, experts)
    loads = [
        pltpu.make_async_copy(src, dst, load_sem.at[at])
        for at, (src, dst) in enumerate(
            ((gate_hbm, gate_ref), (up_hbm, up_ref), (weight_hbm, weight_ref))
        )
    ]
    for load in loads:
        load.start()
    barrier = pltpu.get_barrier_semaphore()
    others = [
        (m, k, f)
        for m in range(columns)
        for k in range(experts)
        for f in range(cores)
        if m or k or f
    ]
    for m, k, f in others:
        pl.semaphore_signal(
            barrier, inc=1, device_id=(flip(d, m), flip(e, k), flip(t, f)), device_id_type=MESH
        )

    chosen = [ids_ref[k : k + 1, :] for k in range(2)]
    routes = [routes_ref[k : k + 1, :].astype(jnp.float32) for k in range(2)]
    row_at = lax.broadcasted_iota(jnp.int32, (tokens, tokens), 0)
    col_at = lax.broadcasted_iota(jnp.int32, (tokens, tokens), 1)
    lower = (row_at < col_at).astype(jnp.bfloat16)
    padded = -(-experts // 16) * 16
    expert_at = lax.broadcasted_iota(jnp.int32, (padded, tokens), 0)
    named = ((expert_at == chosen[0]) | (expert_at == chosen[1])).astype(jnp.float32)
    earlier = jnp.dot(named.astype(jnp.bfloat16), lower, preferred_element_type=jnp.float32)
    position = [
        jnp.sum(jnp.where(expert_at == chosen[k], earlier, 0.0), axis=0, keepdims=True).astype(
            jnp.int32
        )
        for k in range(2)
    ]
    seq_ids = seq_ref[...]
    seq_weights = seq_weight_ref[...]
    token_weight = jnp.zeros((1, tokens), jnp.float32)
    for s in range(seq_weights.shape[1]):
        token_weight = jnp.where(seq_ids == s, seq_weights[0:1, s : s + 1], token_weight)
    weight_column = jnp.sum(jnp.where(row_at == col_at, token_weight, 0.0), axis=1, keepdims=True)
    scaled = (weight_column * grad_ref[...].astype(jnp.float32)).astype(jnp.bfloat16)
    slot_at = lax.broadcasted_iota(jnp.int32, (capacity, tokens), 0)
    group_at = lax.broadcasted_iota(jnp.int32, (group, tokens), 0)
    own_base = e * capacity
    for k in range(experts):
        other = flip(e, k)
        key = jnp.where(
            chosen[0] == other, position[0], jnp.where(chosen[1] == other, position[1], -group - 1)
        )
        picks = (slot_at == key).astype(jnp.float32).astype(jnp.bfloat16)
        rows_ref[k] = jnp.dot(picks, scaled, preferred_element_type=jnp.float32).astype(
            jnp.bfloat16
        )
        route = jnp.where(
            chosen[0] == other, routes[0], jnp.where(chosen[1] == other, routes[1], 0.0)
        )
        spots = (group_at == key + own_base).astype(jnp.float32).astype(jnp.bfloat16)
        spread_route = lax.dot_general(
            jnp.broadcast_to(route, (16, tokens)).astype(jnp.bfloat16),
            spots,
            (((1,), (1,)), ((), ())),
            preferred_element_type=jnp.float32,
        )
        prob_send[k] = spread_route[0:1, :]
    pl.semaphore_wait(barrier, len(others))

    copies = Copies(send_sem, recv_sem)
    base = pl.multiple_of(t * half, half)
    mine = pl.ds(base, half)
    along, probs = [None], {}
    for m in range(columns):
        for k in range(experts):
            if m or k:
                probs[m, k] = copies.start(
                    prob_send.at[k], prob_in.at[m, k], (flip(d, m), flip(e, k), t)
                )
    crossing = [[[] for _ in range(experts)] for _ in range(columns)]

    def to_cores(m, k, src, dst):
        for f in range(1, cores):
            crossing[m][k].append(copies.start(src, dst, (d, e, flip(t, f))))

    def send_along():
        for k in range(1, experts):
            along.append(
                copies.start(rows_ref.at[k], gathered.at[d, e, :, mine], (d, flip(e, k), t))
            )

    def silu_rows(first, last):
        def step(i, carry):
            at = pl.ds(pl.multiple_of(i * SILU_ROWS, SILU_ROWS), SILU_ROWS)
            gate = gate_ref[at, :].astype(jnp.float32)
            up = up_ref[at, :].astype(jnp.float32)
            logistic = 0.5 * jnp.tanh(0.5 * gate) + 0.5
            activated = gate * logistic
            derivative = logistic + activated * (1.0 - logistic)
            hidden_ref[at, :] = (activated * up).astype(jnp.bfloat16)
            gate_coef[at, :] = (up * derivative).astype(jnp.bfloat16)
            up_coef[at, :] = activated.astype(jnp.bfloat16)
            return carry

        lax.fori_loop(first // SILU_ROWS, last // SILU_ROWS, step, 0)

    waited = set()

    def prob_row(m, ks):
        total = None
        for k in ks:
            if (m, k) in probs and (m, k) not in waited:
                probs[m, k].wait_recv()
                waited.add((m, k))
            row = prob_in[m, k]
            total = row if total is None else total + row
        return total

    probes = {}
    started = []

    def unit(m, h, final=False):
        near = range(experts // 2)
        far = range(experts // 2, experts)
        for k in far if h else near:
            for copy in crossing[m][k]:
                copy.wait_recv()
        where = flip(d, m)
        side = upper if h == 0 else 1 - upper
        start = pl.multiple_of(side * (group - span), LANES)
        cols = pl.ds(pl.multiple_of(where * group + start, LANES), span)
        prob_new = prob_row(m, far if h else near)
        prob_all = prob_new + prob_row(m, near) if h else prob_new
        part_ref[2] = prob_all
        part_ref[3] = prob_new
        prob_all = part_ref[2, :, pl.ds(start, span)]
        prob_new = part_ref[3, :, pl.ds(start, span)]
        if h == 0:
            inset = span - half_rows
            gap = pl.multiple_of((1 - side) * half_rows, 16)
            body = pl.multiple_of(side * inset, 16)
            if inset:
                window_ref[pl.ds(gap, inset), :] = jnp.zeros((inset, width), jnp.bfloat16)
            for k in range(experts // 2):
                window_ref[pl.ds(pl.multiple_of(body + k * capacity, 16), capacity), :] = gathered[
                    where, side * (experts // 2) + k
                ]
            block = window_ref[...]
        else:
            block = gathered.at[where].reshape(group, width)[pl.ds(start, span), :]
        tile = units // 2
        part = jnp.zeros((1, span), jnp.float32)
        for i in range(2):
            at = pl.ds(i * tile, tile)
            ups = lax.dot_general(
                weight_ref[at, :], block, (((1,), (1,)), ((), ())),
                preferred_element_type=jnp.float32,
            )
            hidden = hidden_ref[at, cols].astype(jnp.float32)
            part = part + jnp.sum(ups * hidden, axis=0, keepdims=True)
            scaled_hidden[at, :] = (hidden * prob_new).astype(jnp.bfloat16)
            grad_hidden = prob_all * ups
            gate_out[at, cols] = (grad_hidden * gate_coef[at, cols].astype(jnp.float32)).astype(
                jnp.bfloat16
            )
            up_out[at, cols] = (grad_hidden * up_coef[at, cols].astype(jnp.float32)).astype(
                jnp.bfloat16
            )
        part_ref[4 + m, :, pl.ds(start, span)] = part
        if h == 1:
            for k in range(experts):
                for f in range(cores):
                    if m or k or f:
                        probes[m, k, f] = copies.start(
                            part_ref.at[4 + m], probe_in.at[m, k, f], (where, flip(e, k), flip(t, f))
                        )
        first = not started
        started.append(True)
        chunk = width // DOWN_CHUNKS
        for j in range(DOWN_CHUNKS):
            at = pl.ds(j * chunk, chunk)
            if h == 0:
                lines = window_ref[:, at]
            else:
                lines = gathered.at[where].reshape(group, width)[pl.ds(start, span), at]
            out = jnp.dot(scaled_hidden[...], lines, preferred_element_type=jnp.float32)
            if not first:
                out = acc_ref[:, at] + out
            if final:
                down_out[:, at] = out.astype(jnp.bfloat16)
            else:
                acc_ref[:, at] = out

    if columns == 4:
        piece = half // 2
        cuts = [pl.ds(pl.multiple_of(base + p * piece, piece), piece) for p in range(2)]
        sent = {}

        def spread(k):
            origin = flip(e, k)
            if k > 0:
                along[k].wait_recv()
            for m, order in ((1, (0, 1)), (2, (1, 0))):
                for p in order:
                    here = gathered.at[d, origin, :, cuts[p]]
                    src = rows_ref.at[0, :, pl.ds(p * piece, piece)] if k == 0 else here
                    sent[k, m, p] = copies.start(src, here, (flip(d, m), e, t))
            whole = gathered.at[d, origin, :, mine]
            to_cores(0, k, rows_ref.at[0] if k == 0 else whole, whole)

        def forward(k):
            origin = flip(e, k)
            for m, p in ((1, 0), (2, 1)):
                sent[k, m, p].wait_recv()
                block = gathered.at[flip(d, m), origin, :, cuts[p]]
                sent[k, 3, p] = copies.start(block, block, (flip(d, 3 - m), e, t))
                to_cores(m, k, block, block)

        def second(k):
            origin = flip(e, k)
            for m, p in ((1, 1), (2, 0)):
                sent[k, m, p].wait_recv()
                block = gathered.at[flip(d, m), origin, :, cuts[p]]
                to_cores(m, k, block, block)

        def finish(k):
            for p in range(2):
                sent[k, 3, p].wait_recv()
                block = gathered.at[flip(d, 3), flip(e, k), :, cuts[p]]
                to_cores(3, k, block, block)

        rounds = units // SILU_ROWS
        cut = rounds * 5 // 8 * SILU_ROWS
        send_along()
        spread(0)
        gathered[d, e, :, mine] = rows_ref[0]
        prob_in[0, 0] = prob_send[0]
        loads[0].wait()
        loads[1].wait()
        silu_rows(0, cut)
        forward(0)
        second(0)
        for k in range(1, experts // 2):
            spread(k)
        silu_rows(cut, units)
        finish(0)
        loads[2].wait()
        unit(0, 0)
        for k in range(1, experts // 2):
            forward(k)
            second(k)
        spread(experts // 2)
        for k in range(1, experts // 2):
            finish(k)
        unit(1, 0)
        for k in range(experts // 2, experts - 1):
            if k > experts // 2:
                spread(k)
            forward(k)
        unit(2, 0)
        for k in range(experts // 2, experts - 1):
            second(k)
        spread(experts - 1)
        unit(3, 0)
        for k in range(experts // 2, experts - 1):
            finish(k)
        unit(0, 1)
        forward(experts - 1)
        second(experts - 1)
        unit(1, 1)
        finish(experts - 1)
        unit(2, 1)
        unit(3, 1, final=True)
    else:
        send_along()
        gathered[d, e, :, mine] = rows_ref[0]
        prob_in[0, 0] = prob_send[0]
        loads[0].wait()
        loads[1].wait()
        silu_rows(0, units)
        for k in range(1, experts):
            along[k].wait_recv()
        mine_group = gathered.at[d, :, :, mine]
        spreads = [
            copies.start(mine_group, mine_group, (flip(d, m), e, t)) for m in range(1, columns)
        ]
        to_cores(0, 0, mine_group, mine_group)
        loads[2].wait()
        for m in range(columns):
            if m:
                spreads[m - 1].wait_recv()
                block = gathered.at[flip(d, m), :, :, mine]
                to_cores(m, 0, block, block)
            unit(m, 0)
            unit(m, 1, final=m == columns - 1)

    probe_in[0, 0, 0] = part_ref[4]
    lines = []
    for k in range(experts):
        total = None
        for m in range(columns):
            for f in range(cores):
                if m or k or f:
                    probes[m, k, f].wait_recv()
                row = probe_in[m, k, f]
                total = row if total is None else total + row
        lines.append(total)
    lines.append(jnp.zeros((-(-experts // 8) * 8 - experts, group), jnp.float32))
    table = jnp.concatenate([line for line in lines if line.shape[0]], axis=0)
    line_at = lax.broadcasted_iota(jnp.int32, (table.shape[0], tokens), 0)
    for k in range(2):
        spots = (group_at == position[k] + own_base).astype(jnp.float32)
        found = jnp.dot(
            table, spots, preferred_element_type=jnp.float32, precision=lax.Precision.HIGHEST
        )
        line = jnp.full((1, tokens), -1, jnp.int32)
        for j in range(experts):
            line = jnp.where(chosen[k] == flip(e, j), j, line)
        probs_out[k : k + 1, :] = jnp.sum(
            jnp.where(line_at == line, found, 0.0), axis=0, keepdims=True
        )
    for copy in copies.made:
        copy.wait_send()


def local(out_grad, seq_ids, seq_weights, expert_ids, route_probs, down_weight, gate_pre, up_pre):
    experts = lax.axis_size("expert")
    columns = lax.axis_size("dp")
    cores = lax.axis_size("tensor")
    tokens, half = out_grad.shape
    units, slots = gate_pre.shape[1:]
    capacity = slots // (columns * experts)
    width = half * cores
    group = experts * capacity
    span = -(-(group // 2) // LANES) * LANES
    amount = copy_count(columns, experts, cores)
    anywhere = pl.BlockSpec(memory_space=pl.ANY)
    inside = pl.BlockSpec(memory_space=pltpu.VMEM)
    bf16, f32 = jnp.bfloat16, jnp.float32
    gate_grad, up_grad, down_grad, grad_probs = pl.pallas_call(
        functools.partial(moe_kernel, columns, experts, cores, capacity),
        out_shape=(
            jax.ShapeDtypeStruct((units, slots), bf16),
            jax.ShapeDtypeStruct((units, slots), bf16),
            jax.ShapeDtypeStruct((units, width), bf16),
            jax.ShapeDtypeStruct((2, tokens), f32),
        ),
        in_specs=[inside] * 5 + [anywhere] * 3,
        out_specs=[inside] * 4,
        scratch_shapes=[
            pltpu.VMEM((columns, experts, capacity, width), bf16),
            pltpu.VMEM((experts, capacity, half), bf16),
            pltpu.VMEM((experts, 1, group), f32),
            pltpu.VMEM((columns, experts, 1, group), f32),
            pltpu.VMEM((units, width), bf16),
            pltpu.VMEM((units, slots), bf16),
            pltpu.VMEM((units, slots), bf16),
            pltpu.VMEM((units, slots), bf16),
            pltpu.VMEM((units, slots), bf16),
            pltpu.VMEM((units, slots), bf16),
            pltpu.VMEM((span, width), bf16),
            pltpu.VMEM((units, span), bf16),
            pltpu.VMEM((units, width), f32),
            pltpu.VMEM((4 + columns, 1, group), f32),
            pltpu.VMEM((columns, experts, cores, 1, group), f32),
            pltpu.SemaphoreType.DMA((3,)),
            pltpu.SemaphoreType.DMA((amount,)),
            pltpu.SemaphoreType.DMA((amount,)),
        ],
        compiler_params=pltpu.CompilerParams(
            collective_id=0, has_side_effects=True, vmem_limit_bytes=VMEM_LIMIT
        ),
        name="moe",
    )(
        expert_ids.T, route_probs.T, seq_ids, seq_weights, out_grad,
        down_weight[0], gate_pre[0], up_pre[0],
    )
    return gate_grad[None], up_grad[None], down_grad[None], grad_probs.T


VMEM_LIMIT = 50 * 1024 * 1024


def solution(mesh):
    return jax.shard_map(
        local,
        mesh=mesh,
        in_specs=(
            P(("dp", "expert"), "tensor"),
            P(("dp", "expert"), None),
            P(("dp", "expert"), None),
            P(("dp", "expert"), None),
            P(("dp", "expert"), None),
            P("expert", ("dp", "tensor"), None),
            P("expert", ("dp", "tensor"), None),
            P("expert", ("dp", "tensor"), None),
        ),
        out_specs=(
            P("expert", ("dp", "tensor"), None),
            P("expert", ("dp", "tensor"), None),
            P("expert", ("dp", "tensor"), None),
            P(("dp", "expert"), None),
        ),
        check_vma=False,
    )
```

time: 88.7 us -> 65.7 us (0.74)
  other arithmetic: 13.9 us -> 0 us
  Pallas kernels: 65.8 us -> 53 us
  local copies, waits for them, and re-layouts: 6.4 us -> 11.8 us
  matrix products: 1.59 us -> 0 us
    pallas_call x1, Pallas kernels: 65.8 us -> 53 us  [local(): pl.pallas_call(functools.partial(moe_kernel, columns, experts, cores, cap...]
    broadcast_in_dim x2 -> x0, other arithmetic: 12.1 us -> none  [local(): return (gate_out[None], up_out[None], grad_w[None], grad_probs)]
    unnamed x8 -> x18, local copies, waits for them, and re-layouts: 3.82 us -> 11.8 us
    dot_general x2 -> x0, matrix products: 1.59 us -> none  [the longest x1 1.39 us: local(): jnp.dot(picks, scaled, preferred_element_type=jnp.float32)]
    convert_element_type x4 -> x0, local copies, waits for them, and re-layouts: 1.1 us -> none  [the longest x2 0.91 us: local(): route_probs.reshape(-1).astype(jnp.float32)[None, :]]
    reduce_sum x3 -> x0, other arithmetic: 1.04 us -> none  [the longest x1 0.75 us: local(): weight_tok = jnp.sum(member * seq_weights[0][None, :], axis=1)]
where the time goes in v1:
time: 65.7 us; the launch traced here: 65.5 us
  Pallas kernels  53 us (81%)
  local copies, waits for them, and re-layouts  11.8 us (18%)
  between operations  0.67 us (1%)
    pallas_call x1, Pallas kernels, local(): pl.pallas_call(functools.partial(moe_kernel, columns, experts, cores, cap...  53 us
    unnamed x18, local copies, waits for them, and re-layouts  11.8 us

profile of v1, /device:TPU:0, one launch (start us, length us, event | category | flops | bytes accessed | tf_op | source)
XLA Modules:
  0.0 65.5 jit_solution(687893121280930408)
XLA Ops:
  0.6 0.0 copy-start
  0.6 0.9 %copy-done = bf16[128,1024]{1,0:T(8,128)(2,1)S(1)} copy-done((bf16[128,1024]{1,0:T(8,128)(2,1)S(1)}, bf16[128,1024]{1,0:T(8,128)(2,1)}, u32[]{:S(2)}) %copy-start) | copy-done | bytes 262168
  1.6 0.0 copy-start.1
  1.6 0.7 %copy-done.1 = s32[128,2]{0,1:T(2,128)S(1)} copy-done((s32[128,2]{0,1:T(2,128)S(1)}, s32[128,2]{0,1:T(2,128)}, u32[]{:S(2)}) %copy-start.1) | copy-done | bytes 1048
  2.3 0.0 copy-start.2
  2.3 0.7 copy-done.2
  2.9 0.0 copy-start.3
  2.9 0.7 copy-done.3
  3.6 0.0 copy-start.4
  3.6 0.7 copy-done.4
  4.2 53.0 %moe.1 = (bf16[896,1536]{1,0:T(8,128)(2,1)S(1)}, bf16[896,1536]{1,0:T(8,128)(2,1)}, bf16[896,2048]{1,0:T(8,128)(2,1)}, f32[2,128]{1,0:T(2,128)S(1)}) custom-call(s32[2,128]{1,0:T(2,128)S(1)} %bitcast.11, bf16[2,128]{1,0:T(2,128)(2,1)S(1)} %bitcast.12, s32[1,128]{1,0:T(1,128)S(1)} %copy-done.3, f32[1,4]{1,0:T(1,128)S(1)} %copy-done.4, ...), custom_call_target="tpu_custom_call" | custom-call | tf_op jit(solution)/shard_map/moe/pallas_call | solution.py:434
  57.3 0.0 copy-start.6
  57.3 1.5 %copy.16 = bf16[1,896,1536]{2,1,0:T(8,128)(2,1)} copy(bf16[1,896,1536]{2,1,0:T(8,128)(2,1)S(1)} %bitcast.9) | data formatting | bytes 5505024
  58.8 1.2 %copy-done.6 = bf16[896,1536]{1,0:T(8,128)(2,1)S(1)} copy-done((bf16[896,1536]{1,0:T(8,128)(2,1)S(1)}, bf16[896,1536]{1,0:T(8,128)(2,1)}, u32[]{:S(2)}) %copy-start.6) | copy-done | bytes 2752536
  60.0 0.0 copy-start.5
  60.0 1.5 %copy.17 = bf16[1,896,1536]{2,1,0:T(8,128)(2,1)} copy(bf16[1,896,1536]{2,1,0:T(8,128)(2,1)S(1)} %bitcast.15) | data formatting | bytes 5505024
  61.6 1.5 %copy-done.5 = bf16[896,2048]{1,0:T(8,128)(2,1)S(1)} copy-done((bf16[896,2048]{1,0:T(8,128)(2,1)S(1)}, bf16[896,2048]{1,0:T(8,128)(2,1)}, u32[]{:S(2)}) %copy-start.5) | copy-done | bytes 3670040
  63.1 1.8 %copy.18 = bf16[1,896,2048]{2,1,0:T(8,128)(2,1)} copy(bf16[1,896,2048]{2,1,0:T(8,128)(2,1)S(1)} %bitcast.13) | data formatting | bytes 7340032
  64.9 0.6 copy.19
Async XLA Ops:
  0.6 1.0 %copy-start = (bf16[128,1024]{1,0:T(8,128)(2,1)S(1)}, bf16[128,1024]{1,0:T(8,128)(2,1)}, u32[]{:S(2)}) copy-start(bf16[128,1024]{1,0:T(8,128)(2,1)} %grad_ref.1) | copy-start | bytes 786436
  1.6 0.7 %copy-start.1 = (s32[128,2]{0,1:T(2,128)S(1)}, s32[128,2]{0,1:T(2,128)}, u32[]{:S(2)}) copy-start(s32[128,2]{0,1:T(2,128)} %param.11) | copy-start | bytes 3076
  2.3 0.7 %copy-start.2 = (bf16[128,2]{0,1:T(2,128)(2,1)S(1)}, bf16[128,2]{0,1:T(2,128)(2,1)}, u32[]{:S(2)}) copy-start(bf16[128,2]{0,1:T(2,128)(2,1)} %param.12) | copy-start | bytes 1540
  2.9 0.7 %copy-start.3 = (s32[1,128]{1,0:T(1,128)S(1)}, s32[1,128]{1,0:T(1,128)}, u32[]{:S(2)}) copy-start(s32[1,128]{1,0:T(1,128)} %seq_ref.1) | copy-start | bytes 1540
  3.6 0.7 %copy-start.4 = (f32[1,4]{1,0:T(1,128)S(1)}, f32[1,4]{1,0:T(1,128)}, u32[]{:S(2)}) copy-start(f32[1,4]{1,0:T(1,128)} %seq_weight_ref.1) | copy-start | bytes 52
  57.3 2.8 %copy-start.6 = (bf16[896,1536]{1,0:T(8,128)(2,1)S(1)}, bf16[896,1536]{1,0:T(8,128)(2,1)}, u32[]{:S(2)}) copy-start(bf16[896,1536]{1,0:T(8,128)(2,1)} %get-tuple-element.9) | copy-start | bytes 8257540
  60.0 3.0 %copy-start.5 = (bf16[896,2048]{1,0:T(8,128)(2,1)S(1)}, bf16[896,2048]{1,0:T(8,128)(2,1)}, u32[]{:S(2)}) copy-start(bf16[896,2048]{1,0:T(8,128)(2,1)} %get-tuple-element.10) | copy-start | bytes 11010052

commit v2 on v1

--- a/solution.py
+++ b/solution.py
@@ -26,9 +26,8 @@
     def __init__(self, send_sem, recv_sem):
         self.send_sem, self.recv_sem, self.made = send_sem, recv_sem, []
 
-    def start(self, src, dst, device):
-        at = len(self.made)
-        copy = pltpu.make_async_remote_copy(
+    def make(self, at, src, dst, device):
+        return pltpu.make_async_remote_copy(
             src_ref=src,
             dst_ref=dst,
             send_sem=self.send_sem.at[at],
@@ -36,6 +35,9 @@
             device_id=device,
             device_id_type=MESH,
         )
+
+    def start(self, src, dst, device):
+        copy = self.make(len(self.made), src, dst, device)
         copy.start()
         self.made.append(copy)
         return copy
@@ -53,18 +55,26 @@
     experts,
     cores,
     capacity,
+    ids_hbm,
+    routes_hbm,
+    seq_hbm,
+    seq_weight_hbm,
+    grad_hbm,
+    weight_hbm,
+    gate_hbm,
+    up_hbm,
+    gate_low,
+    gate_high,
+    up_low,
+    up_high,
+    down_low,
+    down_high,
+    probs_out,
     ids_ref,
     routes_ref,
     seq_ref,
     seq_weight_ref,
     grad_ref,
-    weight_hbm,
-    gate_hbm,
-    up_hbm,
-    gate_out,
-    up_out,
-    down_out,
-    probs_out,
     gathered,
     rows_ref,
     prob_send,
@@ -73,8 +83,6 @@
     gate_ref,
     up_ref,
     hidden_ref,
-    gate_coef,
-    up_coef,
     window_ref,
     scaled_hidden,
     acc_ref,
@@ -89,17 +97,25 @@
     width = half * cores
     group = experts * capacity
     units = weight_ref.shape[0]
-    slots = gate_ref.shape[1]
     half_rows = group // 2
     span = -(-half_rows // LANES) * LANES
     upper = lax.div(2 * e, experts)
     loads = [
         pltpu.make_async_copy(src, dst, load_sem.at[at])
         for at, (src, dst) in enumerate(
-            ((gate_hbm, gate_ref), (up_hbm, up_ref), (weight_hbm, weight_ref))
+            (
+                (gate_hbm, gate_ref),
+                (up_hbm, up_ref),
+                (weight_hbm, weight_ref),
+                (ids_hbm, ids_ref),
+                (routes_hbm, routes_ref),
+                (seq_hbm, seq_ref),
+                (seq_weight_hbm, seq_weight_ref),
+                (grad_hbm, grad_ref),
+            )
         )
     ]
-    for load in loads:
+    for load in loads[3:] + loads[:3]:
         load.start()
     barrier = pltpu.get_barrier_semaphore()
     others = [
@@ -114,6 +130,8 @@
             barrier, inc=1, device_id=(flip(d, m), flip(e, k), flip(t, f)), device_id_type=MESH
         )
 
+    for load in loads[3:]:
+        load.wait()
     chosen = [ids_ref[k : k + 1, :] for k in range(2)]
     routes = [routes_ref[k : k + 1, :].astype(jnp.float32) for k in range(2)]
     row_at = lax.broadcasted_iota(jnp.int32, (tokens, tokens), 0)
@@ -130,10 +148,9 @@
         for k in range(2)
     ]
     seq_ids = seq_ref[...]
-    seq_weights = seq_weight_ref[...]
     token_weight = jnp.zeros((1, tokens), jnp.float32)
-    for s in range(seq_weights.shape[1]):
-        token_weight = jnp.where(seq_ids == s, seq_weights[0:1, s : s + 1], token_weight)
+    for s in range(seq_weight_ref.shape[1]):
+        token_weight = jnp.where(seq_ids == s, seq_weight_ref[0:1, s : s + 1], token_weight)
     weight_column = jnp.sum(jnp.where(row_at == col_at, token_weight, 0.0), axis=1, keepdims=True)
     scaled = (weight_column * grad_ref[...].astype(jnp.float32)).astype(jnp.bfloat16)
     slot_at = lax.broadcasted_iota(jnp.int32, (capacity, tokens), 0)
@@ -164,7 +181,7 @@
     copies = Copies(send_sem, recv_sem)
     base = pl.multiple_of(t * half, half)
     mine = pl.ds(base, half)
-    along, probs = [None], {}
+    probs = {}
     for m in range(columns):
         for k in range(experts):
             if m or k:
@@ -177,11 +194,16 @@
         for f in range(1, cores):
             crossing[m][k].append(copies.start(src, dst, (d, e, flip(t, f))))
 
-    def send_along():
-        for k in range(1, experts):
-            along.append(
-                copies.start(rows_ref.at[k], gathered.at[d, e, :, mine], (d, flip(e, k), t))
-            )
+    first_along = len(copies.made)
+
+    def along(k, at=None):
+        place = first_along + (k if at is None else at) - 1
+        return copies.make(
+            place, rows_ref.at[k], gathered.at[d, e, :, mine], (d, flip(e, k), t)
+        )
+
+    for k in range(1, experts):
+        copies.made.append(along(k))
 
     def silu_rows(first, last):
         def step(i, carry):
@@ -192,8 +214,8 @@
             activated = gate * logistic
             derivative = logistic + activated * (1.0 - logistic)
             hidden_ref[at, :] = (activated * up).astype(jnp.bfloat16)
-            gate_coef[at, :] = (up * derivative).astype(jnp.bfloat16)
-            up_coef[at, :] = activated.astype(jnp.bfloat16)
+            gate_ref[at, :] = (up * derivative).astype(jnp.bfloat16)
+            up_ref[at, :] = activated.astype(jnp.bfloat16)
             return carry
 
         lax.fori_loop(first // SILU_ROWS, last // SILU_ROWS, step, 0)
@@ -213,12 +235,20 @@
     probes = {}
     started = []
 
-    def unit(m, h, final=False):
+    def arrived(m, h):
+        for k in range(experts // 2 * h, experts // 2 * (h + 1)) if columns == 4 else range(1):
+            for copy in crossing[m][k]:
+                copy.wait_recv()
+            crossing[m][k] = []
+
+    def unit(m, h):
+        with jax.named_scope(f"unit{m}{h}"):
+            arrived(m, h)
+            unit_down([unit_up(m, h, 0)])
+
+    def unit_up(m, h, place):
         near = range(experts // 2)
         far = range(experts // 2, experts)
-        for k in far if h else near:
-            for copy in crossing[m][k]:
-                copy.wait_recv()
         where = flip(d, m)
         side = upper if h == 0 else 1 - upper
         start = pl.multiple_of(side * (group - span), LANES)
@@ -252,12 +282,12 @@
             )
             hidden = hidden_ref[at, cols].astype(jnp.float32)
             part = part + jnp.sum(ups * hidden, axis=0, keepdims=True)
-            scaled_hidden[at, :] = (hidden * prob_new).astype(jnp.bfloat16)
+            scaled_hidden[place, at, :] = (hidden * prob_new).astype(jnp.bfloat16)
             grad_hidden = prob_all * ups
-            gate_out[at, cols] = (grad_hidden * gate_coef[at, cols].astype(jnp.float32)).astype(
+            (gate_low, gate_high)[i][:, cols] = (grad_hidden * gate_ref[at, cols].astype(jnp.float32)).astype(
                 jnp.bfloat16
             )
-            up_out[at, cols] = (grad_hidden * up_coef[at, cols].astype(jnp.float32)).astype(
+            (up_low, up_high)[i][:, cols] = (grad_hidden * up_ref[at, cols].astype(jnp.float32)).astype(
                 jnp.bfloat16
             )
         part_ref[4 + m, :, pl.ds(start, span)] = part
@@ -268,32 +298,45 @@
                         probes[m, k, f] = copies.start(
                             part_ref.at[4 + m], probe_in.at[m, k, f], (where, flip(e, k), flip(t, f))
                         )
-        first = not started
-        started.append(True)
+        return where, start, h, place
+
+    def unit_down(items, final=False):
         chunk = width // DOWN_CHUNKS
-        for j in range(DOWN_CHUNKS):
-            at = pl.ds(j * chunk, chunk)
-            if h == 0:
-                lines = window_ref[:, at]
-            else:
-                lines = gathered.at[where].reshape(group, width)[pl.ds(start, span), at]
-            out = jnp.dot(scaled_hidden[...], lines, preferred_element_type=jnp.float32)
-            if not first:
-                out = acc_ref[:, at] + out
-            if final:
-                down_out[:, at] = out.astype(jnp.bfloat16)
-            else:
-                acc_ref[:, at] = out
+        tile = units // 2
+        for where, start, h, place in items:
+            first = not started
+            started.append(True)
+            for j in range(DOWN_CHUNKS):
+                at = pl.ds(j * chunk, chunk)
+                if h == 0:
+                    lines = window_ref[:, at]
+                else:
+                    lines = gathered.at[where].reshape(group, width)[pl.ds(start, span), at]
+                out = jnp.dot(scaled_hidden[place], lines, preferred_element_type=jnp.float32)
+                if not first:
+                    out = acc_ref[:, at] + out
+                if final and place == items[-1][-1]:
+                    down_low[:, at] = out[:tile].astype(jnp.bfloat16)
+                    down_high[:, at] = out[tile:].astype(jnp.bfloat16)
+                else:
+                    acc_ref[:, at] = out
 
     if columns == 4:
         piece = half // 2
         cuts = [pl.ds(pl.multiple_of(base + p * piece, piece), piece) for p in range(2)]
         sent = {}
 
+        middle = lax.div(e * (3 - e), 2)
+        masks, origins = list(range(experts)), [flip(e, k) for k in range(experts)]
+        if experts == 4:
+            swap = middle * (origins[3] - origins[2])
+            masks[2], masks[3] = 2 + middle, 3 - middle
+            origins[2], origins[3] = origins[2] + swap, origins[3] - swap
+
         def spread(k):
-            origin = flip(e, k)
+            origin = origins[k]
             if k > 0:
-                along[k].wait_recv()
+                along(k, masks[k]).wait_recv()
             for m, order in ((1, (0, 1)), (2, (1, 0))):
                 for p in order:
                     here = gathered.at[d, origin, :, cuts[p]]
@@ -303,7 +346,7 @@
             to_cores(0, k, rows_ref.at[0] if k == 0 else whole, whole)
 
         def forward(k):
-            origin = flip(e, k)
+            origin = origins[k]
             for m, p in ((1, 0), (2, 1)):
                 sent[k, m, p].wait_recv()
                 block = gathered.at[flip(d, m), origin, :, cuts[p]]
@@ -311,7 +354,7 @@
                 to_cores(m, k, block, block)
 
         def second(k):
-            origin = flip(e, k)
+            origin = origins[k]
             for m, p in ((1, 1), (2, 0)):
                 sent[k, m, p].wait_recv()
                 block = gathered.at[flip(d, m), origin, :, cuts[p]]
@@ -320,60 +363,74 @@
         def finish(k):
             for p in range(2):
                 sent[k, 3, p].wait_recv()
-                block = gathered.at[flip(d, 3), flip(e, k), :, cuts[p]]
+                block = gathered.at[flip(d, 3), origins[k], :, cuts[p]]
                 to_cores(3, k, block, block)
 
-        rounds = units // SILU_ROWS
-        cut = rounds * 5 // 8 * SILU_ROWS
-        send_along()
+        def send_far(place, order):
+            if experts == 4:
+
+                @pl.when(middle == place)
+                def _():
+                    for k in order:
+                        along(k).start()
+
+            elif place == 0:
+                for k in range(2, experts):
+                    along(k).start()
+
+        near, last = experts // 2, experts - 1
+        along(1).start()
         spread(0)
+        send_far(1, (3, 2))
         gathered[d, e, :, mine] = rows_ref[0]
         prob_in[0, 0] = prob_send[0]
         loads[0].wait()
         loads[1].wait()
-        silu_rows(0, cut)
+        silu_rows(0, units)
         forward(0)
         second(0)
-        for k in range(1, experts // 2):
+        for k in range(1, near):
             spread(k)
-        silu_rows(cut, units)
-        finish(0)
         loads[2].wait()
         unit(0, 0)
-        for k in range(1, experts // 2):
+        send_far(0, (3, 2))
+        finish(0)
+        for k in range(1, near):
             forward(k)
+        for k in range(near, last):
+            spread(k)
+        for k in range(1, near):
             second(k)
-        spread(experts // 2)
-        for k in range(1, experts // 2):
+        unit(1, 0)
+        for k in range(1, near):
             finish(k)
-        unit(1, 0)
-        for k in range(experts // 2, experts - 1):
-            if k > experts // 2:
-                spread(k)
+        for k in range(near, last):
             forward(k)
+        spread(last)
         unit(2, 0)
-        for k in range(experts // 2, experts - 1):
+        for k in range(near, last):
             second(k)
-        spread(experts - 1)
         unit(3, 0)
-        for k in range(experts // 2, experts - 1):
+        for k in range(near, last):
             finish(k)
+        forward(last)
         unit(0, 1)
-        forward(experts - 1)
-        second(experts - 1)
+        second(last)
         unit(1, 1)
-        finish(experts - 1)
-        unit(2, 1)
-        unit(3, 1, final=True)
+        finish(last)
+        arrived(2, 1)
+        arrived(3, 1)
+        unit_down([unit_up(2, 1, 0), unit_up(3, 1, 1)], final=True)
     else:
-        send_along()
+        for k in range(1, experts):
+            along(k).start()
         gathered[d, e, :, mine] = rows_ref[0]
         prob_in[0, 0] = prob_send[0]
         loads[0].wait()
         loads[1].wait()
         silu_rows(0, units)
         for k in range(1, experts):
-            along[k].wait_recv()
+            along(k).wait_recv()
         mine_group = gathered.at[d, :, :, mine]
         spreads = [
             copies.start(mine_group, mine_group, (flip(d, m), e, t)) for m in range(1, columns)
@@ -386,7 +443,7 @@
                 block = gathered.at[flip(d, m), :, :, mine]
                 to_cores(m, 0, block, block)
             unit(m, 0)
-            unit(m, 1, final=m == columns - 1)
+            unit_down([unit_up(m, 1, 0)], final=m == columns - 1)
 
     probe_in[0, 0, 0] = part_ref[4]
     lines = []
@@ -417,6 +474,29 @@
         copy.wait_send()
 
 
+def finish_kernel(*refs):
+    parts, probs_ref, wholes, probs_hbm, sem = refs[:6], refs[6], refs[7:10], refs[10], refs[11]
+    stores = [pltpu.make_async_copy(probs_ref, probs_hbm, sem.at[6])]
+    for at, part in enumerate(parts):
+        rows = part.shape[0]
+        whole = wholes[at // 2].at[pl.ds(at % 2 * rows, rows), :]
+        stores.append(pltpu.make_async_copy(part, whole, sem.at[at]))
+    for store in stores:
+        store.start()
+    for store in stores:
+        store.wait()
+
+
+def size_of(shapes):
+    total = 0
+    for shape in shapes:
+        elements = 1
+        for extent in shape.shape:
+            elements *= extent
+        total += elements * jnp.dtype(shape.dtype).itemsize
+    return total
+
+
 def local(out_grad, seq_ids, seq_weights, expert_ids, route_probs, down_weight, gate_pre, up_pre):
     experts = lax.axis_size("expert")
     columns = lax.axis_size("dp")
@@ -428,51 +508,80 @@
     group = experts * capacity
     span = -(-(group // 2) // LANES) * LANES
     amount = copy_count(columns, experts, cores)
-    anywhere = pl.BlockSpec(memory_space=pl.ANY)
+    hbm = pl.BlockSpec(memory_space=pltpu.HBM)
     inside = pl.BlockSpec(memory_space=pltpu.VMEM)
     bf16, f32 = jnp.bfloat16, jnp.float32
-    gate_grad, up_grad, down_grad, grad_probs = pl.pallas_call(
+    wholes = [
+        jax.ShapeDtypeStruct((units, slots), bf16),
+        jax.ShapeDtypeStruct((units, slots), bf16),
+        jax.ShapeDtypeStruct((units, width), bf16),
+    ]
+    tail = [jax.ShapeDtypeStruct((2, tokens), f32)]
+    results = [
+        jax.ShapeDtypeStruct((units // 2, whole.shape[1]), bf16) for whole in wholes for _ in range(2)
+    ] + tail
+    scratch = [
+        pltpu.VMEM((2, tokens), jnp.int32),
+        pltpu.VMEM((2, tokens), bf16),
+        pltpu.VMEM((1, tokens), jnp.int32),
+        pltpu.VMEM(seq_weights.shape, f32),
+        pltpu.VMEM((tokens, half), bf16),
+        pltpu.VMEM((columns, experts, capacity, width), bf16),
+        pltpu.VMEM((experts, capacity, half), bf16),
+        pltpu.VMEM((experts, 1, group), f32),
+        pltpu.VMEM((columns, experts, 1, group), f32),
+        pltpu.VMEM((units, width), bf16),
+        pltpu.VMEM((units, slots), bf16),
+        pltpu.VMEM((units, slots), bf16),
+        pltpu.VMEM((units, slots), bf16),
+        pltpu.VMEM((span, width), bf16),
+        pltpu.VMEM((2, units, span), bf16),
+        pltpu.VMEM((units, width), f32),
+        pltpu.VMEM((4 + columns, 1, group), f32),
+        pltpu.VMEM((columns, experts, cores, 1, group), f32),
+    ]
+    passed = pl.pallas_call(
         functools.partial(moe_kernel, columns, experts, cores, capacity),
-        out_shape=(
-            jax.ShapeDtypeStruct((units, slots), bf16),
-            jax.ShapeDtypeStruct((units, slots), bf16),
-            jax.ShapeDtypeStruct((units, width), bf16),
-            jax.ShapeDtypeStruct((2, tokens), f32),
-        ),
-        in_specs=[inside] * 5 + [anywhere] * 3,
-        out_specs=[inside] * 4,
-        scratch_shapes=[
-            pltpu.VMEM((columns, experts, capacity, width), bf16),
-            pltpu.VMEM((experts, capacity, half), bf16),
-            pltpu.VMEM((experts, 1, group), f32),
-            pltpu.VMEM((columns, experts, 1, group), f32),
-            pltpu.VMEM((units, width), bf16),
-            pltpu.VMEM((units, slots), bf16),
-            pltpu.VMEM((units, slots), bf16),
-            pltpu.VMEM((units, slots), bf16),
-            pltpu.VMEM((units, slots), bf16),
-            pltpu.VMEM((units, slots), bf16),
-            pltpu.VMEM((span, width), bf16),
-            pltpu.VMEM((units, span), bf16),
-            pltpu.VMEM((units, width), f32),
-            pltpu.VMEM((4 + columns, 1, group), f32),
-            pltpu.VMEM((columns, experts, cores, 1, group), f32),
-            pltpu.SemaphoreType.DMA((3,)),
+        out_shape=results,
+        in_specs=[hbm] * 8,
+        out_specs=[inside] * 7,
+        scratch_shapes=scratch
+        + [
+            pltpu.SemaphoreType.DMA((8,)),
             pltpu.SemaphoreType.DMA((amount,)),
             pltpu.SemaphoreType.DMA((amount,)),
         ],
         compiler_params=pltpu.CompilerParams(
-            collective_id=0, has_side_effects=True, vmem_limit_bytes=VMEM_LIMIT
+            collective_id=0,
+            has_side_effects=True,
+            vmem_limit_bytes=max(size_of(results + scratch) + SPARE, LEAST_GRANT),
         ),
         name="moe",
     )(
-        expert_ids.T, route_probs.T, seq_ids, seq_weights, out_grad,
-        down_weight[0], gate_pre[0], up_pre[0],
+        *(
+            pltpu.with_memory_space_constraint(array, pltpu.HBM)
+            for array in (
+                expert_ids.T, route_probs.T, seq_ids, seq_weights, out_grad,
+                down_weight[0], gate_pre[0], up_pre[0],
+            )
+        )
     )
+    gate_grad, up_grad, down_grad, grad_probs = pl.pallas_call(
+        finish_kernel,
+        out_shape=wholes + tail,
+        in_specs=[inside] * 7,
+        out_specs=[hbm] * 4,
+        scratch_shapes=[pltpu.SemaphoreType.DMA((7,))],
+        compiler_params=pltpu.CompilerParams(
+            vmem_limit_bytes=size_of(results) + SPARE
+        ),
+        name="finish",
+    )(*passed)
     return gate_grad[None], up_grad[None], down_grad[None], grad_probs.T
 
 
-VMEM_LIMIT = 50 * 1024 * 1024
+SPARE = 3 * 1024 * 1024
+LEAST_GRANT = 44 * 1024 * 1024
 
 
 def solution(mesh):

time: 65.7 us -> 53.7 us (0.82)
  local copies, waits for them, and re-layouts: 11.8 us -> 0 us
    unnamed x18 -> x0, local copies, waits for them, and re-layouts: 11.8 us -> none
    pallas_call x1, Pallas kernels: 53 us -> 49.1 us  [local(): pl.pallas_call(functools.partial(moe_kernel, columns, experts, cores, cap...]
    pallas_call x0 -> x1, Pallas kernels: none -> 3.66 us  [local(): pl.pallas_call(finish_kernel, out_shape=wholes + tail, in_specs=[inside]...]
where the time goes in v2:
time: 53.7 us; the launch traced here: 53.6 us
  Pallas kernels  52.8 us (98%)
  between operations  0.8 us (1%)
    pallas_call x1, Pallas kernels, local(): pl.pallas_call(functools.partial(moe_kernel, columns, experts, cores, cap...  49.1 us
    pallas_call x1, Pallas kernels, local(): pl.pallas_call(finish_kernel, out_shape=wholes + tail, in_specs=[inside]...  3.66 us

profile of v2, /device:TPU:0, one launch (start us, length us, event | category | flops | bytes accessed | tf_op | source)
XLA Modules:
  0.0 53.6 jit_solution(17495563075272658411)
XLA Ops:
  0.6 49.1 %moe.1 = (bf16[448,1536]{1,0:T(8,128)(2,1)S(1)}, bf16[448,1536]{1,0:T(8,128)(2,1)S(1)}, bf16[448,1536]{1,0:T(8,128)(2,1)S(1)}, bf16[448,1536]{1,0:T(8,128)(2,1)S...) custom-call(s32[2,128]{1,0:T(2,128)} %bitcast.12, ...), custom_call_target="tpu_custom_call" | custom-call | tf_op jit(solution)/shard_map/moe/pallas_call | solution.py:543
  49.8 3.7 %finish.1 = (bf16[896,1536]{1,0:T(8,128)(2,1)}, bf16[896,1536]{1,0:T(8,128)(2,1)}, bf16[896,2048]{1,0:T(8,128)(2,1)}, f32[2,128]{1,0:T(2,128)}) custom-call(bf16[448,1536]{1,0:T(8,128)(2,1)S(1)} %get-tuple-element.15.refs_0_, bf16[448,1536]{1,0:T(8,128)(2,1)S(1)} %get-tuple-element.16.refs_1_, bf16[448,1536]{1,0:T(8,128)(2,1)S(1)} %get-tuple-element.17.refs_2_, ...), custom_call_target="tpu_custom_call" | custom-call | tf_op jit(solution)/shard_map/finish/pallas_call | solution.py:569

commit v3 on v2

--- a/solution.py
+++ b/solution.py
@@ -392,8 +392,10 @@
         for k in range(1, near):
             spread(k)
         loads[2].wait()
-        unit(0, 0)
+        arrived(0, 0)
+        item = unit_up(0, 0, 0)
         send_far(0, (3, 2))
+        unit_down([item])
         finish(0)
         for k in range(1, near):
             forward(k)
@@ -406,21 +408,26 @@
             finish(k)
         for k in range(near, last):
             forward(k)
+        arrived(2, 0)
+        item = unit_up(2, 0, 0)
         spread(last)
-        unit(2, 0)
+        unit_down([item])
         for k in range(near, last):
             second(k)
         unit(3, 0)
         for k in range(near, last):
             finish(k)
+        arrived(0, 1)
+        item = unit_up(0, 1, 0)
         forward(last)
-        unit(0, 1)
+        unit_down([item])
         second(last)
         unit(1, 1)
         finish(last)
         arrived(2, 1)
+        item = unit_up(2, 1, 0)
         arrived(3, 1)
-        unit_down([unit_up(2, 1, 0), unit_up(3, 1, 1)], final=True)
+        unit_down([item, unit_up(3, 1, 1)], final=True)
     else:
         for k in range(1, experts):
             along(k).start()

time: 53.7 us -> 50.5 us (0.940)
  Pallas kernels: 52.8 us -> 49.5 us
    pallas_call x1, Pallas kernels: 49.1 us -> 45.9 us  [local(): pl.pallas_call(functools.partial(moe_kernel, columns, experts, cores, cap...]
where the time goes in v3:
time: 50.5 us; the launch traced here: 50.3 us
  Pallas kernels  49.5 us (98%)
  between operations  0.8 us (2%)
    pallas_call x1, Pallas kernels, local(): pl.pallas_call(functools.partial(moe_kernel, columns, experts, cores, cap...  45.9 us
    pallas_call x1, Pallas kernels, local(): pl.pallas_call(finish_kernel, out_shape=wholes + tail, in_specs=[inside]...  3.66 us

profile of v3, /device:TPU:0, one launch (start us, length us, event | category | flops | bytes accessed | tf_op | source)
XLA Modules:
  0.0 50.3 jit_solution(9008405236392459667)
XLA Ops:
  0.6 45.9 %moe.1 = (bf16[448,1536]{1,0:T(8,128)(2,1)S(1)}, bf16[448,1536]{1,0:T(8,128)(2,1)S(1)}, bf16[448,1536]{1,0:T(8,128)(2,1)S(1)}, bf16[448,1536]{1,0:T(8,128)(2,1)S...) custom-call(s32[2,128]{1,0:T(2,128)} %bitcast.12, ...), custom_call_target="tpu_custom_call" | custom-call | tf_op jit(solution)/shard_map/moe/pallas_call | solution.py:550
  46.5 3.7 %finish.1 = (bf16[896,1536]{1,0:T(8,128)(2,1)}, bf16[896,1536]{1,0:T(8,128)(2,1)}, bf16[896,2048]{1,0:T(8,128)(2,1)}, f32[2,128]{1,0:T(2,128)}) custom-call(bf16[448,1536]{1,0:T(8,128)(2,1)S(1)} %get-tuple-element.15.refs_0_, bf16[448,1536]{1,0:T(8,128)(2,1)S(1)} %get-tuple-element.16.refs_1_, bf16[448,1536]{1,0:T(8,128)(2,1)S(1)} %get-tuple-element.17.refs_2_, ...), custom_call_target="tpu_custom_call" | custom-call | tf_op jit(solution)/shard_map/finish/pallas_call | solution.py:576
